TPU v7x, 32 devices: a whole 2x2x4 slice. The times are simulated.
32 devices in a mesh: grp: 2 (over x), row: 16 (over z, y, core).
Axes of the slice: x: 2, y: 2, z: 4, core: 2. Of those that a mesh axis runs over, the one named last changes fastest.
Arguments:
- prior_basis: float32 [131072, 512], P(('grp', 'row')), parts along dimension 0, may hold values from -1 to 1, as said below
- samples: float32 [4, 131072, 64], P(None, ('grp', 'row')), parts along dimension 1, may hold values from -8 to 8
Outputs:
- new_basis: float32 [131072, 256], P(('grp', 'row')), parts along dimension 0
- leaf_estimates: float32 [4, 512], P(None, ('grp', 'row')), parts along dimension 1
There are 2 independent parts, one for each index of `grp`. A program takes and returns all parts, laid end to end along the dimension named above; each array names one. Nothing has to cross between parts.
Inputs may be any that keep to these rules, and one draw needn't show every extreme that they name: The columns of prior_basis are orthonormal to float32 rounding.
All inputs are finite; a program needn't handle non-finite values.
Results may differ from a plain program's by a relative error of at most 0.0003.
Values sent between devices are 32-bit elements; how exact they have to be, the bound alone decides.
A program may use at most 64 MiB of HBM per device.

v0:
```python
import jax
import jax.numpy as jnp
from jax import lax
from jax.sharding import PartitionSpec as P

LEAF = 256


def local(prior_basis, samples):
    highest = lax.Precision.HIGHEST
    rounds, local_rows, columns = samples.shape
    total_leaves = local_rows // LEAF * lax.axis_size("row")
    new_cols = []
    estimates = []
    for number in range(rounds):
        sample_block = samples[number]
        c_added = None
        if new_cols:
            added = jnp.concatenate(new_cols, axis=1)
        partial_value = (
            jnp.dot(prior_basis.T, sample_block, precision=highest),
            jnp.dot(sample_block.T, sample_block, precision=highest),
        )
        if new_cols:
            partial_value = partial_value + (jnp.dot(added.T, sample_block, precision=highest),)
        summed = lax.psum(partial_value, "row")
        c_prior = summed[0]
        stat = summed[1]
        if new_cols:
            c_added = summed[2]
        remainder = sample_block - jnp.dot(prior_basis, c_prior, precision=highest)
        if new_cols:
            remainder = remainder - jnp.dot(added, c_added, precision=highest)
        gram = stat - jnp.dot(c_prior.T, c_prior, precision=highest)
        if new_cols:
            gram = gram - jnp.dot(c_added.T, c_added, precision=highest)
        energy = jnp.trace(stat)
        factor = jnp.linalg.cholesky(gram)
        fresh_cols = jax.scipy.linalg.solve_triangular(factor, remainder.T, lower=True).T
        leaf_energy = jnp.sum(
            (remainder * remainder).reshape(local_rows // LEAF, LEAF, columns), axis=(1, 2)
        )
        estimates.append(jnp.sqrt(total_leaves * leaf_energy / energy))
        new_cols.append(fresh_cols)
    return (jnp.concatenate(new_cols, axis=1), jnp.stack(estimates))


def solution(mesh):
    in_specs = (P(("grp", "row"), None), P(None, ("grp", "row"), None))
    out_specs = (P(("grp", "row"), None), P(None, ("grp", "row")))
    return jax.shard_map(local, mesh=mesh, in_specs=in_specs, out_specs=out_specs, check_vma=False)
```

profile of v0, /device:TPU:0, one launch (start us, length us, event | category | flops | bytes accessed | tf_op | source)
XLA Modules:
  0.0 476.9 jit_solution(54412126924712377)
XLA Ops:
  7.2 9.8 %fusion.14 = f32[512,64]{0,1:T(8,128)} fusion(f32[4096,512]{1,0:T(8,128)} %param.5, f32[4,4096,64]{1,2,0:T(8,128)} %param.6), kind=kOutput, calls=%fused_computation.34 | convolution fusion | flops 1610612736 | bytes 9568256 | tf_op jit(solution)/shard_map/dot_general | solution.py:21
  17.0 6.1 %fusion.21 = f32[512,64]{0,1:T(8,128)} fusion(f32[4096,512]{1,0:T(8,128)S(1)} %copy-done, f32[4,4096,64]{1,2,0:T(8,128)S(1)} %copy-done.1), kind=kOutput, calls=%fused_computation.41 | convolution fusion | flops 1610612736 | bytes 9568256 | tf_op jit(solution)/shard_map/dot_general | solution.py:21
  23.1 6.3 %fusion.27 = f32[512,64]{0,1:T(8,128)} fusion(f32[4096,512]{1,0:T(8,128)S(1)} %copy-done, f32[4,4096,64]{1,2,0:T(8,128)S(1)} %copy-done.1), kind=kOutput, calls=%fused_computation.47 | convolution fusion | flops 1610612736 | bytes 9568256 | tf_op jit(solution)/shard_map/dot_general | solution.py:21
  29.4 6.1 %fusion.8 = f32[512,64]{0,1:T(8,128)} fusion(f32[4096,512]{1,0:T(8,128)S(1)} %copy-done, f32[4,4096,64]{1,2,0:T(8,128)S(1)} %copy-done.1), kind=kOutput, calls=%fused_computation.28 | convolution fusion | flops 1610612736 | bytes 9568256 | tf_op jit(solution)/shard_map/dot_general | solution.py:21
  35.6 2.5 fusion.23
  38.1 2.7 fusion.29
  40.8 3.1 fusion.10
  43.9 63.6 %psum.77 = f32[64,64]{0,1:T(8,128)S(1)} all-reduce(f32[64,64]{0,1:T(8,128)S(1)} %fusion.29), channel_id=1, replica_groups=mesh['grp'=2,'row'=16] {'row'}, use_global_device_ids=true, to_apply=%region_0.0 | all-reduce | flops 4096 | bytes 32768 | tf_op jit(solution)/shard_map/psum | solution.py:26
  108.1 2.5 fusion.16
  110.7 19.2 %all-reduce.9.cloned.1.call-done = (f32[512,64]{0,1:T(8,128)}, f32[512,64]{0,1:T(8,128)}, f32[512,64]{0,1:T(8,128)}, f32[512,64]{0,1:T(8,128)}) async-done(((f32[512,64]{0,1:T(8,128)}, f32[512,64]{0,1:T(8,128)}, f32[512,64]{0,1:T(8,128)}, f32[512,64]{0,1:T(8,128)}), (f32[512,64]{0,1:T(8,128)}, f32[512,64]{0,1:T(8,128)}, f32[512,64]{0,1:T(8,128)}, f32[512,64]{0,1:T(8,128)})) %all-reduce.9.cloned.1.call-update) | async-done | bytes 524304 | tf_op jit(solution)/shard_map/psum | solution.py:26
  131.1 11.6 %multiply_reduce_fusion.3 = (f32[4096]{0:T(1024)S(1)}, f32[4096,64]{0,1:T(8,128)S(1)}) fusion(f32[512,64]{0,1:T(8,128)} %get-tuple-element.17, f32[4096,512]{1,0:T(8,128)} %param.5, f32[4,4096,64]{1,2,0:T(8,128)} %param.6), kind=kOutput, calls=%fused_computation.54 | convolution fusion | flops 1611395072 | bytes 10633216 | tf_op jit(solution)/shard_map/dot_general | solution.py:31
  142.8 5.8 %cholesky.74 = f32[64,64]{1,0:T(8,128)S(1)} custom-call(f32[64,64]{1,0:T(8,128)S(1)} %fusion.53), custom_call_target="Cholesky" | custom-call | tf_op jit(solution)/shard_map/jit(cholesky)/cholesky | solution.py:38
  150.0 4.9 %custom-call.8 = f32[1,64,64]{1,2,0:T(8,128)S(1)} custom-call(f32[1,64,64]{2,1,0:T(8,128)S(1)} %fusion.42), custom_call_target="InvertDiagBlocksLowerTriangular" | custom-call | tf_op jit(solution)/shard_map/jit(_solve_triangular)/triangular_solve | solution.py:39
  155.9 2.2 fusion.19
  158.1 60.2 %all-reduce.2 = (f32[64,64]{1,0:T(8,128)S(1)}, f32[64,64]{0,1:T(8,128)S(1)}) all-reduce(f32[64,64]{1,0:T(8,128)S(1)} %fusion.19, f32[64,64]{0,1:T(8,128)S(1)} %fusion.23), channel_id=1, replica_groups=mesh['grp'=2,'row'=16] {'row'}, use_global_device_ids=true, to_apply=%region_6.9 | all-reduce | flops 8192 | bytes 65536 | tf_op jit(solution)/shard_map/psum | solution.py:26
  219.3 10.8 %fusion.2 = f32[4096,64]{0,1:T(8,128)S(1)} fusion(f32[512,64]{0,1:T(8,128)S(1)} %copy-done.5, f32[4096,512]{1,0:T(8,128)} %param.5, f32[4,4096,64]{1,2,0:T(8,128)} %param.6), kind=kOutput, calls=%fused_computation.11 | convolution fusion | flops 1610874880 | bytes 10616832 | tf_op jit(solution)/shard_map/dot_general | solution.py:31
  230.1 11.7 %fusion = f32[4096,64]{0,1:T(8,128)} fusion(f32[512,64]{0,1:T(8,128)S(1)} %copy-done.3, f32[4096,512]{1,0:T(8,128)} %param.5, f32[4,4096,64]{1,2,0:T(8,128)} %param.6), kind=kOutput, calls=%fused_computation.5 | convolution fusion | flops 1610874880 | bytes 10616832 | tf_op jit(solution)/shard_map/dot_general | solution.py:31
  242.2 5.8 %cholesky.85 = f32[64,64]{1,0:T(8,128)S(1)} custom-call(f32[64,64]{1,0:T(8,128)S(1)} %fusion.51), custom_call_target="Cholesky" | custom-call | tf_op jit(solution)/shard_map/jit(cholesky)/cholesky | solution.py:38
  249.4 4.9 %custom-call.9 = f32[1,64,64]{1,2,0:T(8,128)S(1)} custom-call(f32[1,64,64]{2,1,0:T(8,128)S(1)} %fusion.43), custom_call_target="InvertDiagBlocksLowerTriangular" | custom-call | tf_op jit(solution)/shard_map/jit(_solve_triangular)/triangular_solve | solution.py:39
  256.7 11.7 %fusion.1 = f32[4096,64]{0,1:T(8,128)} fusion(f32[512,64]{0,1:T(8,128)S(1)} %copy-done.4, f32[4096,512]{1,0:T(8,128)} %param.5, f32[4,4096,64]{1,2,0:T(8,128)} %param.6), kind=kOutput, calls=%fused_computation.8 | convolution fusion | flops 1610874880 | bytes 10616832 | tf_op jit(solution)/shard_map/dot_general | solution.py:31
  269.5 3.6 fusion.5
  273.1 57.9 %all-reduce.1 = (f32[128,64]{0,1:T(8,128)S(1)}, f32[64,64]{0,1:T(8,128)S(1)}) all-reduce(f32[128,64]{0,1:T(8,128)S(1)} %fusion.5, f32[64,64]{0,1:T(8,128)S(1)} %fusion.16), channel_id=1, replica_groups=mesh['grp'=2,'row'=16] {'row'}, use_global_device_ids=true, to_apply=%region_9.12 | all-reduce | flops 12288 | bytes 98304 | tf_op jit(solution)/shard_map/psum | solution.py:26
  331.5 5.8 %cholesky.96 = f32[64,64]{1,0:T(8,128)S(1)} custom-call(f32[64,64]{1,0:T(8,128)S(1)} %fusion.49), custom_call_target="Cholesky" | custom-call | tf_op jit(solution)/shard_map/jit(cholesky)/cholesky | solution.py:38
  338.7 4.9 %custom-call.10 = f32[1,64,64]{1,2,0:T(8,128)S(1)} custom-call(f32[1,64,64]{2,1,0:T(8,128)S(1)} %fusion.44), custom_call_target="InvertDiagBlocksLowerTriangular" | custom-call | tf_op jit(solution)/shard_map/jit(_solve_triangular)/triangular_solve | solution.py:39
  346.1 5.0 %fusion.4 = f32[192,64]{0,1:T(8,128)} fusion(f32[4096,64]{0,1:T(8,128)S(1)} %convolution_bitcast_fusion.2, f32[4096,64]{0,1:T(8,128)S(1)} %convolution_bitcast_fusion.4, f32[4096,64]{0,1:T(8,128)S(1)} %bitcast.142, f32[4,4096,64]{1,2,0:T(8,128)} %param.6), kind=kOutput, calls=%fused_computation.16 | convolution fusion | flops 605552640 | bytes 4243456 | tf_op jit(solution)/shard_map/dot_general | solution.py:25
  353.1 84.2 %all-reduce.7.cloned.1.call-done = (f32[192,64]{0,1:T(8,128)}, f32[64,64]{0,1:T(8,128)}) async-done(((f32[192,64]{0,1:T(8,128)}, f32[64,64]{0,1:T(8,128)}), (f32[192,64]{0,1:T(8,128)}, f32[64,64]{0,1:T(8,128)})) %all-reduce.7.cloned.1.call-update) | async-done | bytes 65552 | tf_op jit(solution)/shard_map/psum | solution.py:26
  440.9 4.5 multiply_reduce_fusion
  445.6 5.8 %cholesky.107 = f32[64,64]{1,0:T(8,128)S(1)} custom-call(f32[64,64]{1,0:T(8,128)S(1)} %fusion.47), custom_call_target="Cholesky" | custom-call | tf_op jit(solution)/shard_map/jit(cholesky)/cholesky | solution.py:38
  452.8 4.9 %custom-call.11 = f32[1,64,64]{1,2,0:T(8,128)S(1)} custom-call(f32[1,64,64]{2,1,0:T(8,128)S(1)} %fusion.45), custom_call_target="InvertDiagBlocksLowerTriangular" | custom-call | tf_op jit(solution)/shard_map/jit(_solve_triangular)/triangular_solve | solution.py:39
  457.7 2.3 convolution_bitcast_fusion
  460.0 2.3 pad_maximum_fusion
  462.2 5.6 %copy.35 = f32[4096,256]{1,0:T(8,128)} copy(f32[4096,256]{0,1:T(8,128)} %pad_maximum_fusion) | data formatting | bytes 8388608
  (67 shorter events, 23.7 us)
Async XLA Ops:
  7.2 122.7 %all-reduce.9.cloned.1.call-start = ((), (), s32[]{:S(2)}) async-start(), calls=%async_computation.1 | async-start | bytes 1048576 | tf_op jit(solution)/shard_map/psum | solution.py:26
  7.2 9.8 %copy-start = (f32[4096,512]{1,0:T(8,128)S(1)}, f32[4096,512]{1,0:T(8,128)}, u32[]{:S(2)}) copy-start(f32[4096,512]{1,0:T(8,128)} %param.5) | copy-start | bytes 25165828
  7.2 9.8 %copy-start.1 = (f32[4,4096,64]{1,2,0:T(8,128)S(1)}, f32[4,4096,64]{1,2,0:T(8,128)}, u32[]{:S(2)}) copy-start(f32[4,4096,64]{1,2,0:T(8,128)} %param.6) | copy-start | bytes 12582916
  35.5 401.9 %all-reduce.7.cloned.1.call-start = ((), (), s32[]{:S(2)}) async-start(), calls=%async_computation | async-start | bytes 196608 | tf_op jit(solution)/shard_map/psum | solution.py:26
  142.7 76.3 %copy-start.5 = (f32[512,64]{0,1:T(8,128)S(1)}, f32[512,64]{0,1:T(8,128)}, u32[]{:S(2)}) copy-start(f32[512,64]{0,1:T(8,128)} %get-tuple-element.16) | copy-start | bytes 393220
  219.3 10.8 %copy-start.3 = (f32[512,64]{0,1:T(8,128)S(1)}, f32[512,64]{0,1:T(8,128)}, u32[]{:S(2)}) copy-start(f32[512,64]{0,1:T(8,128)} %get-tuple-element.14) | copy-start | bytes 393220
  230.1 26.6 %copy-start.4 = (f32[512,64]{0,1:T(8,128)S(1)}, f32[512,64]{0,1:T(8,128)}, u32[]{:S(2)}) copy-start(f32[512,64]{0,1:T(8,128)} %get-tuple-element.15) | copy-start | bytes 393220
  269.5 74.1 %copy-start.2 = (f32[4096,64]{0,1:T(8,128)S(1)}, f32[4096,64]{0,1:T(8,128)}, u32[]{:S(2)}) copy-start(f32[4096,64]{0,1:T(8,128)} %fusion.1) | copy-start | bytes 3145732
  345.0 6.0 %copy-start.6 = (f32[16]{0:T(128)S(1)}, f32[16]{0:T(128)}, u32[]{:S(2)}) copy-start(f32[16]{0:T(128)} %reduce_sum.72) | copy-start | bytes 196
  345.1 6.0 %copy-start.7 = (f32[16]{0:T(128)S(1)}, f32[16]{0:T(128)}, u32[]{:S(2)}) copy-start(f32[16]{0:T(128)} %reduce_sum.76) | copy-start | bytes 196
Sparse Core Ops, SparseCore 0:
  35.7 94.1 all-reduce.8
  351.2 86.1 all-reduce.6
where the time goes:
time: 486 us; the launch traced here: 477 us
  blocking collectives  182 us (37%)
  matrix products  112 us (23%)
  waiting for transfers between devices  103 us (21%)
  other arithmetic  58.5 us (12%)
  between operations  14.8 us (3%)
  local copies, waits for them, and re-layouts  5.95 us (1%)
    psum x3, blocking collectives, local(): summed = lax.psum(partial_value, 'row')  182 us
    psum x2, waiting for transfers between devices, local(): summed = lax.psum(partial_value, 'row')  103 us
    dot_general x4, matrix products, local(): remainder = sample_block - jnp.dot(prior_basis, c_prior, precision=highest)  45.8 us
    dot_general x4, matrix products, local(): jnp.dot(prior_basis.T, sample_block, precision=highest)  28.3 us
    another operation x12, other arithmetic, local(): factor = jnp.linalg.cholesky(gram)  26.1 us
    another operation x8, other arithmetic, local(): jax.scipy.linalg.solve_triangular(factor, remainder.T, lower=True)  22.2 us
    dot_general x4, matrix products, local(): jnp.dot(sample_block.T, sample_block, precision=highest)  10.9 us
    dot_general x3, matrix products, local(): jnp.dot(added.T, sample_block, precision=highest)  10.8 us
  transfers between devices with their start and end apart: 2, of which 2 were waited for; matrix products, arithmetic and copies ran while one was open for 3% of the time, Pallas kernels for 0%

commit v1 on v0

v1 whole, which is shorter than its diff:
```python
import functools

import jax
import jax.numpy as jnp
from jax import lax
from jax.experimental import pallas as pl
from jax.experimental.pallas import tpu as pltpu
from jax.sharding import PartitionSpec as P

LEAF = 256
TILE = 512
F32 = jnp.float32
BF16 = jnp.bfloat16
NN = (((1,), (0,)), ((), ()))
NT = (((1,), (1,)), ((), ()))
TN = (((0,), (0,)), ((), ()))


def split(x):
    hi = x.astype(BF16)
    return hi, (x - hi.astype(F32)).astype(BF16)


def dot(a, b, dims=NN):
    return lax.dot_general(a, b, dims, preferred_element_type=F32)


def exact(a, b, dims=NN):
    return lax.dot_general(
        a, b, dims, precision=lax.Precision.HIGHEST, preferred_element_type=F32
    )


def stats_kernel(p_ref, s_ref, o_ref):
    rounds = s_ref.shape[0]
    basis = p_ref.shape[1]

    @pl.when(pl.program_id(0) == 0)
    def _():
        o_ref[...] = jnp.zeros_like(o_ref)

    st = jnp.concatenate([s_ref[r].T for r in range(rounds)], axis=0)
    sh, sl = split(st)
    ph, plo = split(p_ref[...])
    o_ref[:, :basis] += dot(sh, ph) + dot(sl, ph) + dot(sh, plo)
    o_ref[:, basis:] += dot(sh, sh, NT) + dot(sl, sh, NT) + dot(sh, sl, NT)


def factor_block(block):
    size = block.shape[0]
    width = 2 * size
    groups = size // 8
    eye = (
        lax.broadcasted_iota(jnp.int32, (size, size), 0)
        == lax.broadcasted_iota(jnp.int32, (size, size), 1)
    ).astype(F32)
    aug = jnp.concatenate([block, eye], axis=1)
    rows = [aug[8 * g : 8 * g + 8, :] for g in range(groups)]
    sub = lax.broadcasted_iota(jnp.int32, (8, width), 0)
    for p in range(groups):
        cols = {
            g: [
                jnp.broadcast_to(rows[g][:, 8 * p + j : 8 * p + j + 1], (8, width))
                for j in range(8)
            ]
            for g in range(p, groups)
        }
        v = rows[p]
        scale = jnp.zeros((8, width), F32)
        scaled = []
        for k in range(8):
            d = cols[p][k][k : k + 1, :]
            rinv = 1.0 / d
            scale = jnp.where(sub == k, jnp.broadcast_to(lax.rsqrt(d), (8, width)), scale)
            vk = v[k : k + 1, :] * rinv
            scaled.append(vk)
            below = jnp.where(sub > k, cols[p][k], 0.0)
            steps = {j: cols[p][j][k : k + 1, :] * rinv for j in range(k + 1, 8)}
            for j in range(k + 1, 8):
                cols[p][j] = cols[p][j] - below * steps[j]
            v = v - below * vk
            for g in range(p + 1, groups):
                for j in range(k + 1, 8):
                    cols[g][j] = cols[g][j] - cols[g][k] * steps[j]
        for g in range(p + 1, groups):
            for k in range(8):
                rows[g] = rows[g] - cols[g][k] * scaled[k]
        rows[p] = v * scale
    return jnp.concatenate(rows, axis=0)


def factor_kernel(columns, x_ref, w_ref, lt_ref, e_ref, ae_ref):
    total = x_ref.shape[0]
    basis = x_ref.shape[1] - total
    rounds = total // columns
    ct = x_ref[:, :basis]
    g = x_ref[:, basis:]
    row = lax.broadcasted_iota(jnp.int32, (total, total), 0)
    col = lax.broadcasted_iota(jnp.int32, (total, total), 1)
    eye = row == col
    diag = jnp.sum(jnp.where(eye, g, 0.0), axis=1, keepdims=True)
    for r in range(rounds):
        e_ref[r : r + 1, :] = jnp.broadcast_to(
            jnp.sum(diag[r * columns : (r + 1) * columns, :], axis=0, keepdims=True),
            (1, e_ref.shape[1]),
        )
    ae_ref[:, :total] = g - exact(ct, ct, NT)
    ae_ref[:, total:] = eye.astype(F32)
    lt_ref[...] = jnp.zeros_like(lt_ref)
    for r in range(rounds):
        lo, hi = r * columns, (r + 1) * columns
        both = factor_block(ae_ref[lo:hi, lo:hi])
        upper = (
            lax.broadcasted_iota(jnp.int32, (columns, columns), 0)
            <= lax.broadcasted_iota(jnp.int32, (columns, columns), 1)
        )
        lt_ref[lo:hi, lo:hi] = jnp.where(upper, both[:, :columns], 0.0)
        z = exact(both[:, columns:], ae_ref[lo:hi, :])
        ae_ref[lo:hi, :] = z
        if r + 1 < rounds:
            ae_ref[hi:, :] -= exact(z[:, hi:total], z, TN)
    linv = ae_ref[:, total:]
    w_ref[:, :basis] = -exact(linv, ct)
    w_ref[:, basis:] = linv


def final_kernel(total_leaves, columns, p_ref, s_ref, w_ref, lt_ref, e_ref, n_ref, q_ref, wh, wl, lh, ll, sums):
    rounds = s_ref.shape[0]
    tile, basis = p_ref.shape
    step = pl.program_id(0)
    per = tile // LEAF

    @pl.when(step == 0)
    def _():
        h, l = split(w_ref[...])
        wh[...] = h
        wl[...] = l
        h, l = split(lt_ref[...])
        lh[...] = h
        ll[...] = l

    s = jnp.concatenate([s_ref[r] for r in range(rounds)], axis=1)
    sh, sl = split(s)
    ph, plo = split(p_ref[...])
    ah, al = wh[:, :basis], wl[:, :basis]
    bh, bl = wh[:, basis:], wl[:, basis:]
    out = (
        dot(ph, ah, NT) + dot(plo, ah, NT) + dot(ph, al, NT)
        + dot(sh, bh, NT) + dot(sl, bh, NT) + dot(sh, bl, NT)
    )
    n_ref[...] = out
    nh, nl = split(out)
    rem = dot(nh, lh[...]) + dot(nl, lh[...]) + dot(nh, ll[...])
    sq = rem * rem
    for i in range(per):
        sums[pl.ds(step * per + i, 1), :] = jnp.sum(
            sq[i * LEAF : (i + 1) * LEAF, :], axis=0, keepdims=True
        )

    @pl.when(step == pl.num_programs(0) - 1)
    def _():
        width = rounds * columns
        pick = (
            lax.broadcasted_iota(jnp.int32, (rounds, width), 1) // columns
            == lax.broadcasted_iota(jnp.int32, (rounds, width), 0)
        ).astype(F32)
        leaf = exact(pick, sums[...], NT)
        q_ref[...] = jnp.sqrt(total_leaves * leaf / e_ref[:rounds, :1])


def local(prior_basis, samples):
    rounds, rows, columns = samples.shape
    basis = prior_basis.shape[1]
    total = rounds * columns
    tile = min(TILE, rows)
    leaves = rows // LEAF
    total_leaves = leaves * lax.axis_size("row")
    grid = (rows // tile,)
    p_spec = pl.BlockSpec((tile, basis), lambda i: (i, 0))
    s_spec = pl.BlockSpec((rounds, tile, columns), lambda i: (0, i, 0))
    whole = lambda *shape: pl.BlockSpec(shape, lambda i: (0,) * len(shape))
    part = pl.pallas_call(
        stats_kernel,
        grid=grid,
        in_specs=[p_spec, s_spec],
        out_specs=whole(total, basis + total),
        out_shape=jax.ShapeDtypeStruct((total, basis + total), F32),
        name="stats",
    )(prior_basis, samples)
    stat = lax.psum(part, "row")
    w, lt, energy = pl.pallas_call(
        functools.partial(factor_kernel, columns),
        out_shape=(
            jax.ShapeDtypeStruct((total, basis + total), F32),
            jax.ShapeDtypeStruct((total, total), F32),
            jax.ShapeDtypeStruct((8, 128), F32),
        ),
        scratch_shapes=[pltpu.VMEM((total, 2 * total), F32)],
        name="factor",
    )(stat)
    return pl.pallas_call(
        functools.partial(final_kernel, total_leaves, columns),
        grid=grid,
        in_specs=[p_spec, s_spec, whole(total, basis + total), whole(total, total), whole(8, 128)],
        out_specs=(pl.BlockSpec((tile, total), lambda i: (i, 0)), whole(rounds, leaves)),
        out_shape=(
            jax.ShapeDtypeStruct((rows, total), F32),
            jax.ShapeDtypeStruct((rounds, leaves), F32),
        ),
        scratch_shapes=[
            pltpu.VMEM((total, basis + total), BF16),
            pltpu.VMEM((total, basis + total), BF16),
            pltpu.VMEM((total, total), BF16),
            pltpu.VMEM((total, total), BF16),
            pltpu.VMEM((leaves, total), F32),
        ],
        name="final",
    )(prior_basis, samples, w, lt, energy)


def solution(mesh):
    in_specs = (P(("grp", "row"), None), P(None, ("grp", "row"), None))
    out_specs = (P(("grp", "row"), None), P(None, ("grp", "row")))
    return jax.shard_map(local, mesh=mesh, in_specs=in_specs, out_specs=out_specs, check_vma=False)
```

time: 486 us -> 157 us (0.32); the launches traced: 477 us -> 156 us
  blocking collectives: 182 us -> 0 us
  matrix products: 112 us -> 0 us
  other arithmetic: 58.5 us -> 0 us
  Pallas kernels: 0 us -> 39.9 us
  waiting for transfers between devices: 103 us -> 95.5 us
    psum x3 -> x0, blocking collectives: 182 us -> none  [local(): summed = lax.psum(partial_value, 'row')]
    dot_general x25 -> x0, matrix products: 107 us -> none  [the longest x4 45.8 us: local(): remainder = sample_block - jnp.dot(prior_basis, c_prior, precision=highest)]
    another operation x21 -> x0, other arithmetic: 48.9 us -> none  [the longest x12 26.1 us: local(): factor = jnp.linalg.cholesky(gram)]
    pallas_call x0 -> x3, Pallas kernels: none -> 39.9 us  [the longest x1 15.4 us: local(): pl.pallas_call(functools.partial(final_kernel, total_leaves, columns), gr...]
    psum x2 -> x1, waiting for transfers between devices: 103 us -> 95.5 us  [local(): stat = lax.psum(part, 'row')]
    another operation x4 -> x0, matrix products: 5.38 us -> none  [local(): jax.scipy.linalg.solve_triangular(factor, remainder.T, lower=True)]
    reduce_sum x8 -> x0, other arithmetic: 4.86 us -> none  [the longest x4 3.33 us: local(): energy = jnp.trace(stat)]
  transfers between devices with their start and end apart: 2 -> 1, of which waited for: 2 -> 1; matrix products, arithmetic and copies ran while one was open for 3% -> 0% of each run, Pallas kernels for 0% -> 0%
where the time goes in v1:
time: 157 us; the launch traced here: 156 us
  waiting for transfers between devices  95.5 us (61%)
  Pallas kernels  39.9 us (25%)
  between operations  14 us (9%)
  local copies, waits for them, and re-layouts  6.89 us (4%)
    psum x1, waiting for transfers between devices, local(): stat = lax.psum(part, 'row')  95.5 us
    pallas_call x1, Pallas kernels, local(): pl.pallas_call(functools.partial(final_kernel, total_leaves, columns), gr...  15.4 us
    pallas_call x1, Pallas kernels, local(): pl.pallas_call(stats_kernel, grid=grid, in_specs=[p_spec, s_spec], out_sp...  12.5 us
    pallas_call x1, Pallas kernels, local(): pl.pallas_call(functools.partial(factor_kernel, columns), out_shape=(jax....  12 us
    unnamed x1, local copies, waits for them, and re-layouts  6.89 us
  transfers between devices with their start and end apart: 1, of which 1 were waited for; matrix products, arithmetic and copies ran while one was open for 0% of the time, Pallas kernels for 0%

profile of v1, /device:TPU:0, one launch (start us, length us, event | category | flops | bytes accessed | tf_op | source)
XLA Modules:
  0.0 156.4 jit_solution(10821310915631663124)
XLA Ops:
  7.2 0.0 all-reduce.2.cloned.1.call-start
  7.2 6.9 %copy.5.s_ref = f32[4,4096,64]{2,1,0:T(8,128)} copy(f32[4,4096,64]{1,2,0:T(8,128)} %param.3) | data formatting | bytes 8388608 | tf_op args[1]
  14.1 12.5 %stats.1 = f32[256,768]{1,0:T(8,128)} custom-call(f32[4096,512]{1,0:T(8,128)} %p_ref.3, f32[4,4096,64]{2,1,0:T(8,128)} %copy.5.s_ref), custom_call_target="tpu_custom_call" | custom-call | tf_op jit(solution)/shard_map/stats/pallas_call | solution.py:182
  26.6 0.0 all-reduce.2.cloned.1.call-update
  26.6 95.5 %all-reduce.2.cloned.1.call-done.x_ref = f32[256,768]{1,0:T(8,128)} async-done(((f32[256,768]{1,0:T(8,128)}), f32[256,768]{1,0:T(8,128)}) %all-reduce.2.cloned.1.call-update) | async-done | bytes 786448 | tf_op jit(solution)/shard_map/psum | solution.py:190
  122.1 12.0 %factor.1 = (f32[256,768]{1,0:T(8,128)}, f32[256,256]{1,0:T(8,128)}, f32[8,128]{1,0:T(8,128)}) custom-call(f32[256,768]{1,0:T(8,128)} %all-reduce.2.cloned.1.call-done.x_ref), custom_call_target="tpu_custom_call" | custom-call | tf_op jit(solution)/shard_map/factor/pallas_call | solution.py:191
  134.1 15.4 %final.1 = (f32[4096,256]{1,0:T(8,128)}, f32[4,16]{1,0:T(4,128)}) custom-call(f32[4096,512]{1,0:T(8,128)} %p_ref.3, f32[4,4096,64]{2,1,0:T(8,128)} %copy.5.s_ref, f32[256,768]{1,0:T(8,128)} %get-tuple-element.5.w_ref, f32[256,256]{1,0:T(8,128)} %get-tuple-element.6.lt_ref, f32[8,128]{1,0:T(8,128)} %get-tuple-element.7.e_ref), custom_call_target="tpu_custom_call" | custom-call | tf_op jit(solution)/shard_map/final/pallas_call | solution.py:201
Async XLA Ops:
  7.2 115.0 %all-reduce.2.cloned.1.call-start = ((), (), s32[]{:S(2)}) async-start(), calls=%async_computation | async-start | bytes 1572864 | tf_op jit(solution)/shard_map/psum | solution.py:190
Sparse Core Ops, SparseCore 0:
  26.8 95.3 all-reduce.1

commit v2 on v1

--- a/solution.py
+++ b/solution.py
@@ -11,6 +11,7 @@
 TILE = 512
 F32 = jnp.float32
 BF16 = jnp.bfloat16
+MESH = pl.DeviceIdType.MESH
 NN = (((1,), (0,)), ((), ()))
 NT = (((1,), (1,)), ((), ()))
 TN = (((0,), (0,)), ((), ()))
@@ -39,11 +40,97 @@
     def _():
         o_ref[...] = jnp.zeros_like(o_ref)
 
-    st = jnp.concatenate([s_ref[r].T for r in range(rounds)], axis=0)
+    st = jnp.concatenate([s_ref[r] for r in range(rounds)], axis=0)
     sh, sl = split(st)
     ph, plo = split(p_ref[...])
     o_ref[:, :basis] += dot(sh, ph) + dot(sl, ph) + dot(sh, plo)
     o_ref[:, basis:] += dot(sh, sh, NT) + dot(sl, sh, NT) + dot(sh, sl, NT)
+
+
+def sum_kernel(m, x_ref, o_ref, pair, part, got, total, pair_send, pair_recv, rs_send, rs_recv, ag_send, ag_recv, fw_send, fw_recv):
+    me = lax.axis_index("row")
+    core = lax.rem(me, 2)
+    chip = me // 2
+    mate = me + 1 - 2 * core
+    offsets = sorted(range(1, m), key=lambda i: abs(i - m // 2))
+    peers = [lax.rem(chip + i, m) for i in offsets]
+
+    barrier = pltpu.get_barrier_semaphore()
+    for device in [mate] + [2 * t + core for t in peers]:
+        pl.semaphore_signal(barrier, inc=1, device_id={"row": device}, device_id_type=MESH)
+    pl.semaphore_wait(barrier, m)
+
+    def copy(src, dst, send, recv, device):
+        return pltpu.make_async_remote_copy(
+            src_ref=src, dst_ref=dst, send_sem=send, recv_sem=recv,
+            device_id={"row": device}, device_id_type=MESH,
+        )
+
+    order = peers + [chip]
+    first = [
+        copy(x_ref.at[2 * t + 1 - core], pair.at[t], pair_send.at[t], pair_recv.at[t], mate)
+        for t in order
+    ]
+    for c in first:
+        c.start()
+    second = []
+    for i, t in enumerate(order):
+        first[i].wait_recv()
+        part[t] = x_ref[2 * t + core] + pair[t]
+        if t is not chip:
+            c = copy(part.at[t], got.at[chip], rs_send.at[t], rs_recv.at[chip], 2 * t + core)
+            c.start()
+            second.append(c)
+
+    def arrived(src, dst, recv):
+        return pltpu.make_async_copy(src, dst, recv)
+
+    value = part[chip]
+    for t in reversed(peers):
+        arrived(got.at[t], got.at[t], rs_recv.at[t]).wait()
+        value = value + got[t]
+    total[...] = value
+    o_ref[me] = value
+    third = [copy(total, o_ref.at[me], ag_send.at[t], ag_recv.at[chip], 2 * t + core) for t in peers]
+    for c in third:
+        c.start()
+    last = [copy(total, o_ref.at[me], fw_send.at[chip], fw_recv.at[chip], mate)]
+    last[0].start()
+    for t in reversed(peers):
+        block = o_ref.at[2 * t + core]
+        arrived(block, block, ag_recv.at[t]).wait()
+        c = copy(block, block, fw_send.at[t], fw_recv.at[t], mate)
+        c.start()
+        last.append(c)
+    for t in order:
+        block = o_ref.at[2 * t + 1 - core]
+        arrived(block, block, fw_recv.at[t]).wait()
+    for c in first + second + third + last:
+        c.wait_send()
+
+
+def all_sum(x):
+    n = lax.axis_size("row")
+    m = n // 2
+    rows, width = x.shape
+    chunk = (rows // n, width)
+    vmem = pl.BlockSpec(memory_space=pltpu.VMEM)
+    out = pl.pallas_call(
+        functools.partial(sum_kernel, m),
+        in_specs=[vmem],
+        out_specs=vmem,
+        out_shape=jax.ShapeDtypeStruct((n,) + chunk, F32),
+        scratch_shapes=[
+            pltpu.VMEM((m,) + chunk, F32),
+            pltpu.VMEM((m,) + chunk, F32),
+            pltpu.VMEM((m,) + chunk, F32),
+            pltpu.VMEM(chunk, F32),
+        ]
+        + [pltpu.SemaphoreType.DMA((m,))] * 8,
+        compiler_params=pltpu.CompilerParams(collective_id=0, has_side_effects=True),
+        name="all_sum",
+    )(x.reshape((n,) + chunk))
+    return out.reshape(rows, width)
 
 
 def factor_block(block):
@@ -139,7 +226,7 @@
         lh[...] = h
         ll[...] = l
 
-    s = jnp.concatenate([s_ref[r] for r in range(rounds)], axis=1)
+    s = jnp.concatenate([s_ref[r] for r in range(rounds)], axis=0).T
     sh, sl = split(s)
     ph, plo = split(p_ref[...])
     ah, al = wh[:, :basis], wl[:, :basis]
@@ -177,7 +264,8 @@
     total_leaves = leaves * lax.axis_size("row")
     grid = (rows // tile,)
     p_spec = pl.BlockSpec((tile, basis), lambda i: (i, 0))
-    s_spec = pl.BlockSpec((rounds, tile, columns), lambda i: (0, i, 0))
+    samples = jnp.swapaxes(samples, 1, 2)
+    s_spec = pl.BlockSpec((rounds, columns, tile), lambda i: (0, 0, i))
     whole = lambda *shape: pl.BlockSpec(shape, lambda i: (0,) * len(shape))
     part = pl.pallas_call(
         stats_kernel,
@@ -187,7 +275,7 @@
         out_shape=jax.ShapeDtypeStruct((total, basis + total), F32),
         name="stats",
     )(prior_basis, samples)
-    stat = lax.psum(part, "row")
+    stat = all_sum(part)
     w, lt, energy = pl.pallas_call(
         functools.partial(factor_kernel, columns),
         out_shape=(

time: 157 us -> 68.7 us (0.44)
  waiting for transfers between devices: 95.5 us -> 0 us
  Pallas kernels: 39.9 us -> 67.5 us
  between operations: 14 us -> 0.64 us
  local copies, waits for them, and re-layouts: 6.89 us -> 0 us
    psum x1 -> x0, waiting for transfers between devices: 95.5 us -> none  [local(): stat = lax.psum(part, 'row')]
    pallas_call x0 -> x1, Pallas kernels: none -> 30.2 us  [all_sum(): pl.pallas_call(functools.partial(sum_kernel, m), in_specs=[vmem], out_spe...]
    unnamed x1 -> x0, local copies, waits for them, and re-layouts: 6.89 us -> none
    pallas_call x1, Pallas kernels: 12.5 us -> 10.7 us  [local(): pl.pallas_call(stats_kernel, grid=grid, in_specs=[p_spec, s_spec], out_sp...]
  transfers between devices with their start and end apart: 1 -> 0, of which waited for: 1 -> 0; matrix products, arithmetic and copies ran while one was open for 0% -> 0% of each run, Pallas kernels for 0% -> 0%
where the time goes in v2:
time: 68.7 us; the launch traced here: 68.1 us
  Pallas kernels  67.5 us (98%)
    pallas_call x1, Pallas kernels, all_sum(): pl.pallas_call(functools.partial(sum_kernel, m), in_specs=[vmem], out_spe...  30.2 us
    pallas_call x1, Pallas kernels, local(): pl.pallas_call(functools.partial(final_kernel, total_leaves, columns), gr...  14.6 us
    pallas_call x1, Pallas kernels, local(): pl.pallas_call(functools.partial(factor_kernel, columns), out_shape=(jax....  12 us
    pallas_call x1, Pallas kernels, local(): pl.pallas_call(stats_kernel, grid=grid, in_specs=[p_spec, s_spec], out_sp...  10.7 us

profile of v2, /device:TPU:0, one launch (start us, length us, event | category | flops | bytes accessed | tf_op | source)
XLA Modules:
  0.0 68.1 jit_solution(8106494356018738732)
XLA Ops:
  0.6 10.7 %stats.1 = f32[256,768]{1,0:T(8,128)} custom-call(f32[4096,512]{1,0:T(8,128)} %p_ref.3, f32[4,64,4096]{2,1,0:T(8,128)} %bitcast.3), custom_call_target="tpu_custom_call" | custom-call | tf_op jit(solution)/shard_map/stats/pallas_call | solution.py:270
  11.3 30.2 %all_sum.1 = f32[16,16,768]{2,1,0:T(8,128)} custom-call(f32[16,16,768]{2,1,0:T(8,128)} %bitcast.5), custom_call_target="tpu_custom_call" | custom-call | tf_op jit(solution)/shard_map/all_sum/pallas_call | solution.py:118
  41.6 12.0 %factor.1 = (f32[256,768]{1,0:T(8,128)}, f32[256,256]{1,0:T(8,128)}, f32[8,128]{1,0:T(8,128)}) custom-call(f32[256,768]{1,0:T(8,128)} %bitcast.6), custom_call_target="tpu_custom_call" | custom-call | tf_op jit(solution)/shard_map/factor/pallas_call | solution.py:279
  53.5 14.6 %final.1 = (f32[4096,256]{1,0:T(8,128)}, f32[4,16]{1,0:T(4,128)}) custom-call(f32[4096,512]{1,0:T(8,128)} %p_ref.3, f32[4,64,4096]{2,1,0:T(8,128)} %bitcast.4, f32[256,768]{1,0:T(8,128)} %get-tuple-element.5.w_ref, f32[256,256]{1,0:T(8,128)} %get-tuple-element.6.lt_ref, f32[8,128]{1,0:T(8,128)} %get-tuple-element.7.e_ref), custom_call_target="tpu_custom_call" | custom-call | tf_op jit(solution)/shard_map/final/pallas_call | solution.py:289

commit v3 on v1

--- a/solution.py
+++ b/solution.py
@@ -8,9 +8,11 @@
 from jax.sharding import PartitionSpec as P
 
 LEAF = 256
+LANES = 128
 TILE = 512
 F32 = jnp.float32
 BF16 = jnp.bfloat16
+MESH = pl.DeviceIdType.MESH
 NN = (((1,), (0,)), ((), ()))
 NT = (((1,), (1,)), ((), ()))
 TN = (((0,), (0,)), ((), ()))
@@ -31,19 +33,143 @@
     )
 
 
+def blocks(total, basis):
+    n, b = total // LANES, basis // LANES
+    return [(i, j) for i in range(n) for j in range(b)] + [
+        (i, b + j) for i in range(n) for j in range(i + 1)
+    ]
+
+
+def unpack(x_ref, total, basis):
+    place = {k: i for i, k in enumerate(blocks(total, basis))}
+    n, b = total // LANES, basis // LANES
+
+    def block(i, j):
+        if j >= b and j - b > i:
+            return block(j - b, b + i).T
+        k = place[i, j]
+        return x_ref[k * LANES : (k + 1) * LANES, :]
+
+    full = [[block(i, j) for j in range(b + n)] for i in range(n)]
+    rows = [jnp.concatenate(line, axis=1) for line in full]
+    out = jnp.concatenate(rows, axis=0)
+    return out[:, :basis], out[:, basis:]
+
+
 def stats_kernel(p_ref, s_ref, o_ref):
-    rounds = s_ref.shape[0]
+    rounds, columns = s_ref.shape[:2]
     basis = p_ref.shape[1]
 
     @pl.when(pl.program_id(0) == 0)
     def _():
         o_ref[...] = jnp.zeros_like(o_ref)
 
-    st = jnp.concatenate([s_ref[r].T for r in range(rounds)], axis=0)
+    st = jnp.concatenate([s_ref[r] for r in range(rounds)], axis=0)
     sh, sl = split(st)
     ph, plo = split(p_ref[...])
-    o_ref[:, :basis] += dot(sh, ph) + dot(sl, ph) + dot(sh, plo)
-    o_ref[:, basis:] += dot(sh, sh, NT) + dot(sl, sh, NT) + dot(sh, sl, NT)
+    c = dot(sh, ph) + dot(sl, ph) + dot(sh, plo)
+    g = dot(sh, sh, NT) + dot(sl, sh, NT) + dot(sh, sl, NT)
+    x = jnp.concatenate([c, g], axis=1)
+    for k, (i, j) in enumerate(blocks(rounds * columns, basis)):
+        o_ref[k * LANES : (k + 1) * LANES, :] += x[
+            i * LANES : (i + 1) * LANES, j * LANES : (j + 1) * LANES
+        ]
+
+
+def sum_kernel(line, x_ref, o_ref, pair, mine, theirs, beside, ready, got, total, pair_send, pair_recv, y_send, y_recv, z_send, z_recv, oz_send, oz_recv, oy_send, oy_recv, oc_send, oc_recv):
+    me = lax.axis_index("row")
+    core = lax.rem(me, 2)
+    y = lax.rem(me // 2, 2)
+    z = me // 4
+    mate = me + 1 - 2 * core
+    next_y = me + 2 - 4 * y
+    offsets = sorted(range(1, line), key=lambda i: abs(i - line // 2))
+    peers = [lax.rem(z + i, line) for i in offsets]
+    order = peers + [z]
+
+    def device(t):
+        return 4 * t + 2 * y + core
+
+    barrier = pltpu.get_barrier_semaphore()
+    for other in [mate, next_y] + [device(t) for t in peers]:
+        pl.semaphore_signal(barrier, inc=1, device_id={"row": other}, device_id_type=MESH)
+    pl.semaphore_wait(barrier, line + 1)
+
+    started = []
+
+    def send(src, dst, send_sem, recv_sem, other):
+        c = pltpu.make_async_remote_copy(
+            src_ref=src, dst_ref=dst, send_sem=send_sem, recv_sem=recv_sem,
+            device_id={"row": other}, device_id_type=MESH,
+        )
+        c.start()
+        started.append(c)
+
+    def arrived(block, recv_sem):
+        pltpu.make_async_copy(block, block, recv_sem).wait()
+
+    for t in order:
+        send(x_ref.at[1 - core, :, t], pair.at[:, t], pair_send.at[t], pair_recv.at[t], mate)
+    for t in order:
+        arrived(pair.at[:, t], pair_recv.at[t])
+        theirs[t] = x_ref[core, 1 - y, t] + pair[1 - y, t]
+        mine[t] = x_ref[core, y, t] + pair[y, t]
+        send(theirs.at[t], beside.at[t], y_send.at[t], y_recv.at[t], next_y)
+    for t in peers:
+        arrived(beside.at[t], y_recv.at[t])
+        ready[t] = mine[t] + beside[t]
+        send(ready.at[t], got.at[z], z_send.at[t], z_recv.at[z], device(t))
+    arrived(beside.at[z], y_recv.at[z])
+    value = mine[z] + beside[z]
+    for t in reversed(peers):
+        arrived(got.at[t], z_recv.at[t])
+        value = value + got[t]
+    total[...] = value
+    home = o_ref.at[core, y, z]
+    o_ref[core, y, z] = value
+    for t in peers:
+        send(total, home, oz_send.at[t], oz_recv.at[z], device(t))
+    send(total, home, oy_send.at[z], oy_recv.at[z], next_y)
+    send(total, home, oc_send.at[y, z], oc_recv.at[y, z], mate)
+    back = [z] + list(reversed(peers))
+    for i, t in enumerate(back):
+        if i:
+            block = o_ref.at[core, y, t]
+            arrived(block, oz_recv.at[t])
+            send(block, block, oy_send.at[t], oy_recv.at[t], next_y)
+            send(block, block, oc_send.at[y, t], oc_recv.at[y, t], mate)
+    for t in back:
+        block = o_ref.at[core, 1 - y, t]
+        arrived(block, oy_recv.at[t])
+        send(block, block, oc_send.at[1 - y, t], oc_recv.at[1 - y, t], mate)
+    for t in back:
+        for side in range(2):
+            arrived(o_ref.at[1 - core, side, t], oc_recv.at[side, t])
+    for c in started:
+        c.wait_send()
+
+
+def all_sum(x):
+    n = lax.axis_size("row")
+    line = n // 4
+    rows, width = x.shape
+    chunk = (rows // n, width)
+    vmem = pl.BlockSpec(memory_space=pltpu.VMEM)
+    sem = pltpu.SemaphoreType.DMA
+    out = pl.pallas_call(
+        functools.partial(sum_kernel, line),
+        in_specs=[vmem],
+        out_specs=vmem,
+        out_shape=jax.ShapeDtypeStruct((2, 2, line) + chunk, F32),
+        scratch_shapes=[pltpu.VMEM((2, line) + chunk, F32)]
+        + [pltpu.VMEM((line,) + chunk, F32)] * 5
+        + [pltpu.VMEM(chunk, F32)]
+        + [sem((line,))] * 10
+        + [sem((2, line))] * 2,
+        compiler_params=pltpu.CompilerParams(collective_id=0, has_side_effects=True),
+        name="all_sum",
+    )(x.reshape((2, 2, line) + chunk))
+    return out.reshape(rows, width)
 
 
 def factor_block(block):
@@ -90,11 +216,10 @@
 
 
 def factor_kernel(columns, x_ref, w_ref, lt_ref, e_ref, ae_ref):
-    total = x_ref.shape[0]
-    basis = x_ref.shape[1] - total
+    total = lt_ref.shape[0]
+    basis = w_ref.shape[1] - total
     rounds = total // columns
-    ct = x_ref[:, :basis]
-    g = x_ref[:, basis:]
+    ct, g = unpack(x_ref, total, basis)
     row = lax.broadcasted_iota(jnp.int32, (total, total), 0)
     col = lax.broadcasted_iota(jnp.int32, (total, total), 1)
     eye = row == col
@@ -139,7 +264,7 @@
         lh[...] = h
         ll[...] = l
 
-    s = jnp.concatenate([s_ref[r] for r in range(rounds)], axis=1)
+    s = jnp.concatenate([s_ref[r] for r in range(rounds)], axis=0).T
     sh, sl = split(s)
     ph, plo = split(p_ref[...])
     ah, al = wh[:, :basis], wl[:, :basis]
@@ -172,22 +297,24 @@
     rounds, rows, columns = samples.shape
     basis = prior_basis.shape[1]
     total = rounds * columns
+    packed = LANES * len(blocks(total, basis))
     tile = min(TILE, rows)
     leaves = rows // LEAF
     total_leaves = leaves * lax.axis_size("row")
     grid = (rows // tile,)
     p_spec = pl.BlockSpec((tile, basis), lambda i: (i, 0))
-    s_spec = pl.BlockSpec((rounds, tile, columns), lambda i: (0, i, 0))
+    samples = jnp.swapaxes(samples, 1, 2)
+    s_spec = pl.BlockSpec((rounds, columns, tile), lambda i: (0, 0, i))
     whole = lambda *shape: pl.BlockSpec(shape, lambda i: (0,) * len(shape))
     part = pl.pallas_call(
         stats_kernel,
         grid=grid,
         in_specs=[p_spec, s_spec],
-        out_specs=whole(total, basis + total),
-        out_shape=jax.ShapeDtypeStruct((total, basis + total), F32),
+        out_specs=whole(packed, LANES),
+        out_shape=jax.ShapeDtypeStruct((packed, LANES), F32),
         name="stats",
     )(prior_basis, samples)
-    stat = lax.psum(part, "row")
+    stat = all_sum(part)
     w, lt, energy = pl.pallas_call(
         functools.partial(factor_kernel, columns),
         out_shape=(

time: 157 us -> 66.1 us (0.42)
  waiting for transfers between devices: 95.5 us -> 0 us
  Pallas kernels: 39.9 us -> 64.9 us
  between operations: 14 us -> 0.64 us
  local copies, waits for them, and re-layouts: 6.89 us -> 0 us
    psum x1 -> x0, waiting for transfers between devices: 95.5 us -> none  [local(): stat = lax.psum(part, 'row')]
    pallas_call x0 -> x1, Pallas kernels: none -> 27.6 us  [all_sum(): pl.pallas_call(functools.partial(sum_kernel, line), in_specs=[vmem], out_...]
    unnamed x1 -> x0, local copies, waits for them, and re-layouts: 6.89 us -> none
    pallas_call x1, Pallas kernels: 12.5 us -> 10.7 us  [local(): pl.pallas_call(stats_kernel, grid=grid, in_specs=[p_spec, s_spec], out_sp...]
  transfers between devices with their start and end apart: 1 -> 0, of which waited for: 1 -> 0; matrix products, arithmetic and copies ran while one was open for 0% -> 0% of each run, Pallas kernels for 0% -> 0%
where the time goes in v3:
time: 66.1 us; the launch traced here: 65.5 us
  Pallas kernels  64.9 us (98%)
    pallas_call x1, Pallas kernels, all_sum(): pl.pallas_call(functools.partial(sum_kernel, line), in_specs=[vmem], out_...  27.6 us
    pallas_call x1, Pallas kernels, local(): pl.pallas_call(functools.partial(final_kernel, total_leaves, columns), gr...  14.6 us
    pallas_call x1, Pallas kernels, local(): pl.pallas_call(functools.partial(factor_kernel, columns), out_shape=(jax....  12 us
    pallas_call x1, Pallas kernels, local(): pl.pallas_call(stats_kernel, grid=grid, in_specs=[p_spec, s_spec], out_sp...  10.7 us

profile of v3, /device:TPU:0, one launch (start us, length us, event | category | flops | bytes accessed | tf_op | source)
XLA Modules:
  0.0 65.5 jit_solution(16926246049640180538)
XLA Ops:
  0.6 10.7 %stats.1 = f32[1408,128]{1,0:T(8,128)} custom-call(f32[4096,512]{1,0:T(8,128)} %p_ref.3, f32[4,64,4096]{2,1,0:T(8,128)} %bitcast.3), custom_call_target="tpu_custom_call" | custom-call | tf_op jit(solution)/shard_map/stats/pallas_call | solution.py:309
  11.3 27.6 %all_sum.1 = f32[2,2,4,88,128]{4,3,2,1,0:T(8,128)} custom-call(f32[2,2,4,88,128]{4,3,2,1,0:T(8,128)} %bitcast.6), custom_call_target="tpu_custom_call" | custom-call | tf_op jit(solution)/shard_map/all_sum/pallas_call | solution.py:159
  39.0 12.0 %factor.1 = (f32[256,768]{1,0:T(8,128)}, f32[256,256]{1,0:T(8,128)}, f32[8,128]{1,0:T(8,128)}) custom-call(f32[1408,128]{1,0:T(8,128)} %bitcast.5), custom_call_target="tpu_custom_call" | custom-call | tf_op jit(solution)/shard_map/factor/pallas_call | solution.py:318
  50.9 14.6 %final.1 = (f32[4096,256]{1,0:T(8,128)}, f32[4,16]{1,0:T(4,128)}) custom-call(f32[4096,512]{1,0:T(8,128)} %p_ref.3, f32[4,64,4096]{2,1,0:T(8,128)} %bitcast.4, f32[256,768]{1,0:T(8,128)} %get-tuple-element.5.w_ref, f32[256,256]{1,0:T(8,128)} %get-tuple-element.6.lt_ref, f32[8,128]{1,0:T(8,128)} %get-tuple-element.7.e_ref), custom_call_target="tpu_custom_call" | custom-call | tf_op jit(solution)/shard_map/final/pallas_call | solution.py:328

commit v4 on v3

--- a/solution.py
+++ b/solution.py
@@ -215,82 +215,105 @@
     return jnp.concatenate(rows, axis=0)
 
 
-def factor_kernel(columns, x_ref, w_ref, lt_ref, e_ref, ae_ref):
+def finish_kernel(columns, total_leaves, x_ref, p_hbm, s_hbm, n_hbm, q_ref, p_v, s_v, n_v, ae_ref, lt_ref, xs, ns, wh, wl, lh, ll, sums, p_sem, s_sem, n_sem):
     total = lt_ref.shape[0]
-    basis = w_ref.shape[1] - total
+    rows, basis = p_v.shape
     rounds = total // columns
+    tile = ns.shape[1]
+    chunks = rows // tile
+    depth = basis + total
+
+    def at(i):
+        return slice(i * tile, (i + 1) * tile)
+
+    loads = []
+    for i in range(chunks):
+        loads.append(pltpu.make_async_copy(p_hbm.at[at(i)], p_v.at[at(i)], p_sem.at[i]))
+        loads.append(pltpu.make_async_copy(s_hbm.at[:, :, at(i)], s_v.at[:, :, at(i)], s_sem.at[i]))
+    for c in loads:
+        c.start()
+
     ct, g = unpack(x_ref, total, basis)
     row = lax.broadcasted_iota(jnp.int32, (total, total), 0)
     col = lax.broadcasted_iota(jnp.int32, (total, total), 1)
     eye = row == col
     diag = jnp.sum(jnp.where(eye, g, 0.0), axis=1, keepdims=True)
-    for r in range(rounds):
-        e_ref[r : r + 1, :] = jnp.broadcast_to(
-            jnp.sum(diag[r * columns : (r + 1) * columns, :], axis=0, keepdims=True),
-            (1, e_ref.shape[1]),
-        )
+    energy = jnp.concatenate(
+        [
+            jnp.sum(diag[r * columns : (r + 1) * columns, :], axis=0, keepdims=True)
+            for r in range(rounds)
+        ],
+        axis=0,
+    )
     ae_ref[:, :total] = g - exact(ct, ct, NT)
     ae_ref[:, total:] = eye.astype(F32)
     lt_ref[...] = jnp.zeros_like(lt_ref)
+    upper = (
+        lax.broadcasted_iota(jnp.int32, (columns, columns), 0)
+        <= lax.broadcasted_iota(jnp.int32, (columns, columns), 1)
+    )
     for r in range(rounds):
         lo, hi = r * columns, (r + 1) * columns
         both = factor_block(ae_ref[lo:hi, lo:hi])
-        upper = (
-            lax.broadcasted_iota(jnp.int32, (columns, columns), 0)
-            <= lax.broadcasted_iota(jnp.int32, (columns, columns), 1)
-        )
         lt_ref[lo:hi, lo:hi] = jnp.where(upper, both[:, :columns], 0.0)
         z = exact(both[:, columns:], ae_ref[lo:hi, :])
         ae_ref[lo:hi, :] = z
         if r + 1 < rounds:
             ae_ref[hi:, :] -= exact(z[:, hi:total], z, TN)
     linv = ae_ref[:, total:]
-    w_ref[:, :basis] = -exact(linv, ct)
-    w_ref[:, basis:] = linv
-
-
-def final_kernel(total_leaves, columns, p_ref, s_ref, w_ref, lt_ref, e_ref, n_ref, q_ref, wh, wl, lh, ll, sums):
-    rounds = s_ref.shape[0]
-    tile, basis = p_ref.shape
-    step = pl.program_id(0)
-    per = tile // LEAF
-
-    @pl.when(step == 0)
-    def _():
-        h, l = split(w_ref[...])
-        wh[...] = h
-        wl[...] = l
-        h, l = split(lt_ref[...])
-        lh[...] = h
-        ll[...] = l
-
-    s = jnp.concatenate([s_ref[r] for r in range(rounds)], axis=0).T
-    sh, sl = split(s)
-    ph, plo = split(p_ref[...])
-    ah, al = wh[:, :basis], wl[:, :basis]
-    bh, bl = wh[:, basis:], wl[:, basis:]
-    out = (
-        dot(ph, ah, NT) + dot(plo, ah, NT) + dot(ph, al, NT)
-        + dot(sh, bh, NT) + dot(sl, bh, NT) + dot(sh, bl, NT)
-    )
-    n_ref[...] = out
-    nh, nl = split(out)
-    rem = dot(nh, lh[...]) + dot(nl, lh[...]) + dot(nh, ll[...])
-    sq = rem * rem
-    for i in range(per):
-        sums[pl.ds(step * per + i, 1), :] = jnp.sum(
-            sq[i * LEAF : (i + 1) * LEAF, :], axis=0, keepdims=True
-        )
-
-    @pl.when(step == pl.num_programs(0) - 1)
-    def _():
-        width = rounds * columns
-        pick = (
-            lax.broadcasted_iota(jnp.int32, (rounds, width), 1) // columns
-            == lax.broadcasted_iota(jnp.int32, (rounds, width), 0)
-        ).astype(F32)
-        leaf = exact(pick, sums[...], NT)
-        q_ref[...] = jnp.sqrt(total_leaves * leaf / e_ref[:rounds, :1])
+    wh[:basis], wl[:basis] = split(-exact(linv, ct).T)
+    wh[basis:], wl[basis:] = split(linv.T)
+    lh[...], ll[...] = split(lt_ref[...])
+    for c in loads:
+        c.wait()
+
+    def prepare(i):
+        slot = i % 2
+        h, l = split(p_v[at(i), :])
+        xs[slot, :, :basis] = h
+        xs[slot, :, depth : depth + basis] = l
+        h, l = split(jnp.concatenate([s_v[r, :, at(i)] for r in range(rounds)], axis=0).T)
+        xs[slot, :, basis:depth] = h
+        xs[slot, :, depth + basis :] = l
+
+    def product(i):
+        slot = i % 2
+        h, l = xs[slot, :, :depth], xs[slot, :, depth:]
+        out = dot(h, wh[...]) + dot(l, wh[...]) + dot(h, wl[...])
+        n_v[at(i), :] = out
+        ns[slot, :, :total], ns[slot, :, total:] = split(out)
+
+    def remains(i):
+        slot = i % 2
+        h, l = ns[slot, :, :total], ns[slot, :, total:]
+        rem = dot(h, lh[...]) + dot(l, lh[...]) + dot(h, ll[...])
+        sq = rem * rem
+        for k in range(tile // LEAF):
+            leaf = i * (tile // LEAF) + k
+            sums[leaf : leaf + 1, :] = jnp.sum(
+                sq[k * LEAF : (k + 1) * LEAF, :], axis=0, keepdims=True
+            )
+
+    stores = [
+        pltpu.make_async_copy(n_v.at[at(i)], n_hbm.at[at(i)], n_sem.at[i]) for i in range(chunks)
+    ]
+    prepare(0)
+    for i in range(chunks):
+        product(i)
+        if i + 1 < chunks:
+            prepare(i + 1)
+        if i:
+            stores[i - 1].start()
+            remains(i - 1)
+    stores[-1].start()
+    remains(chunks - 1)
+    pick = (
+        lax.broadcasted_iota(jnp.int32, (rounds, total), 1) // columns
+        == lax.broadcasted_iota(jnp.int32, (rounds, total), 0)
+    ).astype(F32)
+    q_ref[...] = jnp.sqrt(total_leaves * exact(pick, sums[...], NT) / energy)
+    for c in stores:
+        c.wait()
 
 
 def local(prior_basis, samples):
@@ -298,51 +321,54 @@
     basis = prior_basis.shape[1]
     total = rounds * columns
     packed = LANES * len(blocks(total, basis))
-    tile = min(TILE, rows)
+    tile = min(1024, rows)
     leaves = rows // LEAF
     total_leaves = leaves * lax.axis_size("row")
-    grid = (rows // tile,)
-    p_spec = pl.BlockSpec((tile, basis), lambda i: (i, 0))
     samples = jnp.swapaxes(samples, 1, 2)
-    s_spec = pl.BlockSpec((rounds, columns, tile), lambda i: (0, 0, i))
-    whole = lambda *shape: pl.BlockSpec(shape, lambda i: (0,) * len(shape))
     part = pl.pallas_call(
         stats_kernel,
-        grid=grid,
-        in_specs=[p_spec, s_spec],
-        out_specs=whole(packed, LANES),
+        grid=(rows // tile,),
+        in_specs=[
+            pl.BlockSpec((tile, basis), lambda i: (i, 0)),
+            pl.BlockSpec((rounds, columns, tile), lambda i: (0, 0, i)),
+        ],
+        out_specs=pl.BlockSpec((packed, LANES), lambda i: (0, 0)),
         out_shape=jax.ShapeDtypeStruct((packed, LANES), F32),
         name="stats",
     )(prior_basis, samples)
     stat = all_sum(part)
-    w, lt, energy = pl.pallas_call(
-        functools.partial(factor_kernel, columns),
-        out_shape=(
-            jax.ShapeDtypeStruct((total, basis + total), F32),
-            jax.ShapeDtypeStruct((total, total), F32),
-            jax.ShapeDtypeStruct((8, 128), F32),
-        ),
-        scratch_shapes=[pltpu.VMEM((total, 2 * total), F32)],
-        name="factor",
-    )(stat)
+    depth = basis + total
+    chunk = min(TILE, rows)
+    vmem = pl.BlockSpec(memory_space=pltpu.VMEM)
+    hbm = pl.BlockSpec(memory_space=pl.ANY)
+    sem = pltpu.SemaphoreType.DMA((rows // chunk,))
     return pl.pallas_call(
-        functools.partial(final_kernel, total_leaves, columns),
-        grid=grid,
-        in_specs=[p_spec, s_spec, whole(total, basis + total), whole(total, total), whole(8, 128)],
-        out_specs=(pl.BlockSpec((tile, total), lambda i: (i, 0)), whole(rounds, leaves)),
+        functools.partial(finish_kernel, columns, total_leaves),
+        in_specs=[vmem, hbm, hbm],
+        out_specs=(hbm, vmem),
         out_shape=(
             jax.ShapeDtypeStruct((rows, total), F32),
             jax.ShapeDtypeStruct((rounds, leaves), F32),
         ),
         scratch_shapes=[
-            pltpu.VMEM((total, basis + total), BF16),
-            pltpu.VMEM((total, basis + total), BF16),
+            pltpu.VMEM((rows, basis), F32),
+            pltpu.VMEM((rounds, columns, rows), F32),
+            pltpu.VMEM((rows, total), F32),
+            pltpu.VMEM((total, 2 * total), F32),
+            pltpu.VMEM((total, total), F32),
+            pltpu.VMEM((2, chunk, 2 * depth), BF16),
+            pltpu.VMEM((2, chunk, 2 * total), BF16),
+            pltpu.VMEM((depth, total), BF16),
+            pltpu.VMEM((depth, total), BF16),
             pltpu.VMEM((total, total), BF16),
             pltpu.VMEM((total, total), BF16),
             pltpu.VMEM((leaves, total), F32),
+            sem,
+            sem,
+            sem,
         ],
-        name="final",
-    )(prior_basis, samples, w, lt, energy)
+        name="finish",
+    )(stat, prior_basis, samples)
 
 
 def solution(mesh):

time: 66.1 us -> 57.2 us (0.87)
  Pallas kernels: 64.9 us -> 56.4 us
    pallas_call x3 -> x2, Pallas kernels: 37.3 us -> 28.7 us  [the longest x1 19.7 us: local(): pl.pallas_call(functools.partial(finish_kernel, columns, total_leaves), i...]
where the time goes in v4:
time: 57.2 us; the launch traced here: 57 us
  Pallas kernels  56.4 us (99%)
  between operations  0.64 us (1%)
    pallas_call x1, Pallas kernels, all_sum(): pl.pallas_call(functools.partial(sum_kernel, line), in_specs=[vmem], out_...  27.6 us
    pallas_call x1, Pallas kernels, local(): pl.pallas_call(functools.partial(finish_kernel, columns, total_leaves), i...  19.7 us
    pallas_call x1, Pallas kernels, local(): pl.pallas_call(stats_kernel, grid=(rows // tile,), in_specs=[pl.BlockSpec...  8.99 us

profile of v4, /device:TPU:0, one launch (start us, length us, event | category | flops | bytes accessed | tf_op | source)
XLA Modules:
  0.0 57.0 jit_solution(824980453771093166)
XLA Ops:
  0.6 9.0 %stats.1 = f32[1408,128]{1,0:T(8,128)} custom-call(f32[4096,512]{1,0:T(8,128)} %p_hbm.1, f32[4,64,4096]{2,1,0:T(8,128)} %bitcast.3), custom_call_target="tpu_custom_call" | custom-call | tf_op jit(solution)/shard_map/stats/pallas_call | solution.py:328
  9.6 27.6 %all_sum.1 = f32[2,2,4,88,128]{4,3,2,1,0:T(8,128)} custom-call(f32[2,2,4,88,128]{4,3,2,1,0:T(8,128)} %bitcast.6), custom_call_target="tpu_custom_call" | custom-call | tf_op jit(solution)/shard_map/all_sum/pallas_call | solution.py:159
  37.2 19.7 %finish.1 = (f32[4096,256]{1,0:T(8,128)}, f32[4,16]{1,0:T(4,128)}) custom-call(f32[1408,128]{1,0:T(8,128)} %bitcast.5, f32[4096,512]{1,0:T(8,128)} %p_hbm.1, f32[4,64,4096]{2,1,0:T(8,128)} %bitcast.4), custom_call_target="tpu_custom_call" | custom-call | tf_op jit(solution)/shard_map/finish/pallas_call | solution.py:345

commit v5 on v4

--- a/solution.py
+++ b/solution.py
@@ -56,27 +56,7 @@
     return out[:, :basis], out[:, basis:]
 
 
-def stats_kernel(p_ref, s_ref, o_ref):
-    rounds, columns = s_ref.shape[:2]
-    basis = p_ref.shape[1]
-
-    @pl.when(pl.program_id(0) == 0)
-    def _():
-        o_ref[...] = jnp.zeros_like(o_ref)
-
-    st = jnp.concatenate([s_ref[r] for r in range(rounds)], axis=0)
-    sh, sl = split(st)
-    ph, plo = split(p_ref[...])
-    c = dot(sh, ph) + dot(sl, ph) + dot(sh, plo)
-    g = dot(sh, sh, NT) + dot(sl, sh, NT) + dot(sh, sl, NT)
-    x = jnp.concatenate([c, g], axis=1)
-    for k, (i, j) in enumerate(blocks(rounds * columns, basis)):
-        o_ref[k * LANES : (k + 1) * LANES, :] += x[
-            i * LANES : (i + 1) * LANES, j * LANES : (j + 1) * LANES
-        ]
-
-
-def sum_kernel(line, x_ref, o_ref, pair, mine, theirs, beside, ready, got, total, pair_send, pair_recv, y_send, y_recv, z_send, z_recv, oz_send, oz_recv, oy_send, oy_recv, oc_send, oc_recv):
+def sum_kernel(line, p_hbm, s_hbm, o_ref, p_v, s_v, ph, plo, st, acc, x_ref, p_sem, s_sem, pair, mine, theirs, beside, ready, got, total, pair_send, pair_recv, y_send, y_recv, z_send, z_recv, oz_send, oz_recv, oy_send, oy_recv, oc_send, oc_recv):
     me = lax.axis_index("row")
     core = lax.rem(me, 2)
     y = lax.rem(me // 2, 2)
@@ -93,8 +73,61 @@
     barrier = pltpu.get_barrier_semaphore()
     for other in [mate, next_y] + [device(t) for t in peers]:
         pl.semaphore_signal(barrier, inc=1, device_id={"row": other}, device_id_type=MESH)
+    rows, basis = p_v.shape
+    rounds, columns = s_v.shape[:2]
+    width = rounds * columns
+    tile = ph.shape[1]
+    tiles = rows // tile
+
+    def at(i):
+        return slice(i * tile, (i + 1) * tile)
+
+    loads = [
+        (
+            pltpu.make_async_copy(p_hbm.at[at(i)], p_v.at[at(i)], p_sem.at[i]),
+            pltpu.make_async_copy(s_hbm.at[:, :, at(i)], s_v.at[:, :, at(i)], s_sem.at[i]),
+        )
+        for i in range(tiles)
+    ]
+    for one, two in loads:
+        one.start()
+        two.start()
+
+    def prepare(i):
+        slot = i % 2
+        for c in loads[i]:
+            c.wait()
+        ph[slot], plo[slot] = split(p_v[at(i), :])
+        rows_of = jnp.concatenate([s_v[r, :, at(i)] for r in range(rounds)], axis=0)
+        st[slot, :width], st[slot, width:] = split(rows_of)
+
+    prepare(0)
+    for i in range(tiles):
+        slot = i % 2
+        sh, sl = st[slot, :width], st[slot, width:]
+        c = dot(sh, ph[slot]) + dot(sl, ph[slot]) + dot(sh, plo[slot])
+        g = dot(sh, sh, NT) + dot(sl, sh, NT) + dot(sh, sl, NT)
+        if i + 1 < tiles:
+            prepare(i + 1)
+        if i:
+            acc[:, :basis] += c
+            acc[:, basis:] += g
+        else:
+            acc[:, :basis] = c
+            acc[:, basis:] = g
+    high = x_ref.shape[-2]
+    for k, (i, j) in enumerate(blocks(width, basis)):
+        first, end = k * LANES, (k + 1) * LANES
+        while first < end:
+            slot, inside = divmod(first, high)
+            count = min(high - inside, end - first)
+            source = i * LANES + first - k * LANES
+            x_ref[
+                slot // (2 * line), slot // line % 2, slot % line, inside : inside + count, :
+            ] = acc[source : source + count, j * LANES : (j + 1) * LANES]
+            first += count
+
     pl.semaphore_wait(barrier, line + 1)
-
     started = []
 
     def send(src, dst, send_sem, recv_sem, other):
@@ -149,27 +182,42 @@
         c.wait_send()
 
 
-def all_sum(x):
+def all_sum(prior_basis, samples):
     n = lax.axis_size("row")
     line = n // 4
-    rows, width = x.shape
-    chunk = (rows // n, width)
-    vmem = pl.BlockSpec(memory_space=pltpu.VMEM)
+    rounds, columns, rows = samples.shape
+    basis = prior_basis.shape[1]
+    total = rounds * columns
+    packed = LANES * len(blocks(total, basis))
+    chunk = (packed // n, LANES)
+    tile = min(TILE, rows)
+    hbm = pl.BlockSpec(memory_space=pl.ANY)
     sem = pltpu.SemaphoreType.DMA
     out = pl.pallas_call(
         functools.partial(sum_kernel, line),
-        in_specs=[vmem],
-        out_specs=vmem,
+        in_specs=[hbm, hbm],
+        out_specs=pl.BlockSpec(memory_space=pltpu.VMEM),
         out_shape=jax.ShapeDtypeStruct((2, 2, line) + chunk, F32),
-        scratch_shapes=[pltpu.VMEM((2, line) + chunk, F32)]
+        scratch_shapes=[
+            pltpu.VMEM((rows, basis), F32),
+            pltpu.VMEM((rounds, columns, rows), F32),
+            pltpu.VMEM((2, tile, basis), BF16),
+            pltpu.VMEM((2, tile, basis), BF16),
+            pltpu.VMEM((2, 2 * total, tile), BF16),
+            pltpu.VMEM((total, basis + total), F32),
+            pltpu.VMEM((2, 2, line) + chunk, F32),
+            sem((rows // tile,)),
+            sem((rows // tile,)),
+            pltpu.VMEM((2, line) + chunk, F32),
+        ]
         + [pltpu.VMEM((line,) + chunk, F32)] * 5
         + [pltpu.VMEM(chunk, F32)]
         + [sem((line,))] * 10
         + [sem((2, line))] * 2,
         compiler_params=pltpu.CompilerParams(collective_id=0, has_side_effects=True),
         name="all_sum",
-    )(x.reshape((2, 2, line) + chunk))
-    return out.reshape(rows, width)
+    )(prior_basis, samples)
+    return out.reshape(packed, LANES)
 
 
 def factor_block(block):
@@ -195,19 +243,23 @@
         scale = jnp.zeros((8, width), F32)
         scaled = []
         for k in range(8):
-            d = cols[p][k][k : k + 1, :]
+            spread = lambda x: jnp.broadcast_to(x[k : k + 1, :], (8, width))
+            d = spread(cols[p][k])
             rinv = 1.0 / d
-            scale = jnp.where(sub == k, jnp.broadcast_to(lax.rsqrt(d), (8, width)), scale)
-            vk = v[k : k + 1, :] * rinv
-            scaled.append(vk)
+            scale = jnp.where(sub == k, lax.rsqrt(d), scale)
             below = jnp.where(sub > k, cols[p][k], 0.0)
-            steps = {j: cols[p][j][k : k + 1, :] * rinv for j in range(k + 1, 8)}
-            for j in range(k + 1, 8):
-                cols[p][j] = cols[p][j] - below * steps[j]
-            v = v - below * vk
+            heads = {j: spread(cols[p][j]) for j in range(k + 1, 8)}
+            terms = {j: below * heads[j] for j in heads}
+            head = spread(v)
+            term = below * head
+            for j in heads:
+                cols[p][j] = cols[p][j] - terms[j] * rinv
+            v = v - term * rinv
+            scaled.append(head * rinv)
             for g in range(p + 1, groups):
-                for j in range(k + 1, 8):
-                    cols[g][j] = cols[g][j] - cols[g][k] * steps[j]
+                ratio = cols[g][k] * rinv
+                for j in heads:
+                    cols[g][j] = cols[g][j] - ratio * heads[j]
         for g in range(p + 1, groups):
             for k in range(8):
                 rows[g] = rows[g] - cols[g][k] * scaled[k]
@@ -320,23 +372,10 @@
     rounds, rows, columns = samples.shape
     basis = prior_basis.shape[1]
     total = rounds * columns
-    packed = LANES * len(blocks(total, basis))
-    tile = min(1024, rows)
     leaves = rows // LEAF
     total_leaves = leaves * lax.axis_size("row")
     samples = jnp.swapaxes(samples, 1, 2)
-    part = pl.pallas_call(
-        stats_kernel,
-        grid=(rows // tile,),
-        in_specs=[
-            pl.BlockSpec((tile, basis), lambda i: (i, 0)),
-            pl.BlockSpec((rounds, columns, tile), lambda i: (0, 0, i)),
-        ],
-        out_specs=pl.BlockSpec((packed, LANES), lambda i: (0, 0)),
-        out_shape=jax.ShapeDtypeStruct((packed, LANES), F32),
-        name="stats",
-    )(prior_basis, samples)
-    stat = all_sum(part)
+    stat = all_sum(prior_basis, samples)
     depth = basis + total
     chunk = min(TILE, rows)
     vmem = pl.BlockSpec(memory_space=pltpu.VMEM)

time: 57.2 us -> 57.7 us (level)
    pallas_call x1, Pallas kernels: 19.7 us -> 24.2 us  [local(): pl.pallas_call(functools.partial(finish_kernel, columns, total_leaves), i...]
    pallas_call x2 -> x1, Pallas kernels: 36.6 us -> 32.6 us  [all_sum(): pl.pallas_call(functools.partial(sum_kernel, line), in_specs=[hbm, hbm],...]
where the time goes in v5:
time: 57.7 us; the launch traced here: 57.5 us
  Pallas kernels  56.7 us (98%)
  between operations  0.8 us (1%)
    pallas_call x1, Pallas kernels, all_sum(): pl.pallas_call(functools.partial(sum_kernel, line), in_specs=[hbm, hbm],...  32.6 us
    pallas_call x1, Pallas kernels, local(): pl.pallas_call(functools.partial(finish_kernel, columns, total_leaves), i...  24.2 us

profile of v5, /device:TPU:0, one launch (start us, length us, event | category | flops | bytes accessed | tf_op | source)
XLA Modules:
  0.0 57.5 jit_solution(15558585056366157270)
XLA Ops:
  0.6 32.6 %all_sum.1 = f32[2,2,4,88,128]{4,3,2,1,0:T(8,128)} custom-call(f32[4096,512]{1,0:T(8,128)} %p_hbm.3, f32[4,64,4096]{2,1,0:T(8,128)} %bitcast.2), custom_call_target="tpu_custom_call" | custom-call | tf_op jit(solution)/shard_map/all_sum/pallas_call | solution.py:196
  33.2 24.2 %finish.1 = (f32[4096,256]{1,0:T(8,128)}, f32[4,16]{1,0:T(4,128)}) custom-call(f32[1408,128]{1,0:T(8,128)} %bitcast.4, f32[4096,512]{1,0:T(8,128)} %p_hbm.3, f32[4,64,4096]{2,1,0:T(8,128)} %bitcast.3), custom_call_target="tpu_custom_call" | custom-call | tf_op jit(solution)/shard_map/finish/pallas_call | solution.py:384

commit v6 on v5

--- a/solution.py
+++ b/solution.py
@@ -243,23 +243,19 @@
         scale = jnp.zeros((8, width), F32)
         scaled = []
         for k in range(8):
-            spread = lambda x: jnp.broadcast_to(x[k : k + 1, :], (8, width))
-            d = spread(cols[p][k])
+            d = cols[p][k][k : k + 1, :]
             rinv = 1.0 / d
-            scale = jnp.where(sub == k, lax.rsqrt(d), scale)
+            scale = jnp.where(sub == k, jnp.broadcast_to(lax.rsqrt(d), (8, width)), scale)
+            vk = v[k : k + 1, :] * rinv
+            scaled.append(vk)
             below = jnp.where(sub > k, cols[p][k], 0.0)
-            heads = {j: spread(cols[p][j]) for j in range(k + 1, 8)}
-            terms = {j: below * heads[j] for j in heads}
-            head = spread(v)
-            term = below * head
-            for j in heads:
-                cols[p][j] = cols[p][j] - terms[j] * rinv
-            v = v - term * rinv
-            scaled.append(head * rinv)
+            steps = {j: cols[p][j][k : k + 1, :] * rinv for j in range(k + 1, 8)}
+            for j in range(k + 1, 8):
+                cols[p][j] = cols[p][j] - below * steps[j]
+            v = v - below * vk
             for g in range(p + 1, groups):
-                ratio = cols[g][k] * rinv
-                for j in heads:
-                    cols[g][j] = cols[g][j] - ratio * heads[j]
+                for j in range(k + 1, 8):
+                    cols[g][j] = cols[g][j] - cols[g][k] * steps[j]
         for g in range(p + 1, groups):
             for k in range(8):
                 rows[g] = rows[g] - cols[g][k] * scaled[k]

time: 57.7 us -> 53.5 us (0.927)
  Pallas kernels: 56.7 us -> 52.5 us
    pallas_call x1, Pallas kernels: 24.2 us -> 19.9 us  [local(): pl.pallas_call(functools.partial(finish_kernel, columns, total_leaves), i...]
where the time goes in v6:
time: 53.5 us; the launch traced here: 53.3 us
  Pallas kernels  52.5 us (98%)
  between operations  0.8 us (1%)
    pallas_call x1, Pallas kernels, all_sum(): pl.pallas_call(functools.partial(sum_kernel, line), in_specs=[hbm, hbm],...  32.6 us
    pallas_call x1, Pallas kernels, local(): pl.pallas_call(functools.partial(finish_kernel, columns, total_leaves), i...  19.9 us

profile of v6, /device:TPU:0, one launch (start us, length us, event | category | flops | bytes accessed | tf_op | source)
XLA Modules:
  0.0 53.3 jit_solution(14170341715443025486)
XLA Ops:
  0.6 32.6 %all_sum.1 = f32[2,2,4,88,128]{4,3,2,1,0:T(8,128)} custom-call(f32[4096,512]{1,0:T(8,128)} %p_hbm.3, f32[4,64,4096]{2,1,0:T(8,128)} %bitcast.2), custom_call_target="tpu_custom_call" | custom-call | tf_op jit(solution)/shard_map/all_sum/pallas_call | solution.py:196
  33.2 19.9 %finish.1 = (f32[4096,256]{1,0:T(8,128)}, f32[4,16]{1,0:T(4,128)}) custom-call(f32[1408,128]{1,0:T(8,128)} %bitcast.4, f32[4096,512]{1,0:T(8,128)} %p_hbm.3, f32[4,64,4096]{2,1,0:T(8,128)} %bitcast.3), custom_call_target="tpu_custom_call" | custom-call | tf_op jit(solution)/shard_map/finish/pallas_call | solution.py:380
